TPU v7x, 32 devices: a whole 2x2x4 slice. The times are simulated.
32 devices in a mesh: beam: 2 (over x), chan: 16 (over z, y, core).
Axes of the slice: x: 2, y: 2, z: 4, core: 2. Of those that a mesh axis runs over, the one named last changes fastest.
Arguments:
- spectra: float32 [4096, 1024], P(('beam', 'chan')), parts along dimension 0, may hold values from -6 to 6
- chan_delay: int32 [2048, 32], P('chan'), may hold values from 0 to 63
- window_base: int32 [16, 64], P(None, 'chan'), may hold values from 0 to 28
- trial_offset: int32 [256, 64], P('chan'), may hold values from 0 to 3
- shift_blocks: int32 [256], P('chan'), may hold values from 0 to 7
- template_len: int32 [8], replicated, may hold values from 1 to 128
Outputs:
- scores: float32 [512, 8, 1024], P(('beam', 'chan')), parts along dimension 0
There are 2 independent parts, one for each index of `beam`. A program takes and returns all parts, laid end to end along the dimension named above; an argument that names none is the same for every part. Nothing has to cross between parts.
All inputs are finite; a program needn't handle non-finite values.
Results may differ from a plain program's by a relative error of at most 0.0032.
Values may be sent and summed in bfloat16 or wider, within the bound.
No kernel may reach another device: no remote copies, remote signals or barrier semaphores. Data moves between devices by JAX's collectives and lax.ppermute only.
A program may use at most 64 MiB of HBM per device.

v0:
```python
import jax
import jax.numpy as jnp
from jax import lax
from jax.sharding import PartitionSpec as P

SUB_CH = 32
NDELAY = 32
MAXD = 64
SPAN = 4
BLOCK = 128


def make_rows(spectra, chan_delay):
    channels, samples = spectra.shape
    band_count = channels // SUB_CH
    padded = jnp.pad(spectra, ((0, 0), (MAXD, 0)))
    delay_of = jnp.transpose(chan_delay)
    band_of = lax.iota(jnp.int32, channels) // SUB_CH
    same_band = lax.iota(jnp.int32, band_count)[:, None] == band_of[None, :]
    highest = lax.Precision.HIGHEST
    total = jnp.zeros((NDELAY * band_count, samples), jnp.float32)
    for delay in range(MAXD):
        table = (delay_of == delay)[:, None, :] & same_band[None, :, :]
        table = table.astype(jnp.float32).reshape(NDELAY * band_count, channels)
        moved = padded[:, MAXD - delay : MAXD - delay + samples]
        total = total + jnp.dot(table, moved, precision=highest, preferred_element_type=jnp.float32)
    total = total * SUB_CH ** (-0.5)
    return total.astype(jnp.bfloat16).reshape(NDELAY, band_count, samples)


def template_tables(lengths):
    offset_in = lax.iota(jnp.int32, BLOCK)[:, None] - lax.iota(jnp.int32, BLOCK)[None, :]
    length_cube = lengths[:, None, None]
    weight = lax.rsqrt(lengths.astype(jnp.float32))[:, None, None]
    inside = jnp.where((offset_in[None] >= 0) & (offset_in[None] < length_cube), weight, 0.0)
    beyond = jnp.where(offset_in[None] + BLOCK < length_cube, weight, 0.0)
    templates = lengths.shape[0]
    inside = jnp.transpose(inside, (1, 0, 2)).reshape(BLOCK, templates * BLOCK)
    beyond = jnp.transpose(beyond, (1, 0, 2)).reshape(BLOCK, templates * BLOCK)
    return (inside, beyond)


def local(spectra, chan_delay, window_base, trial_offset, shift_blocks, template_len):
    samples = spectra.shape[1]
    delay_rows = make_rows(spectra, chan_delay)
    band_count = delay_rows.shape[1]
    subbands = trial_offset.shape[1]
    trial_count = trial_offset.shape[0]
    windows_index = window_base[:, :, None] + lax.iota(jnp.int32, SPAN)[None, None, :]
    band_index = lax.iota(jnp.int32, band_count)[None, :, None]
    windows = delay_rows[windows_index, band_index]
    received = lax.all_to_all(windows, "chan", split_axis=0, concat_axis=0, tiled=True)
    stacked = received.reshape(subbands * SPAN, samples)
    picker = trial_offset[:, :, None] == lax.iota(jnp.int32, SPAN)[None, None, :]
    picker = picker.astype(jnp.bfloat16).reshape(trial_count, subbands * SPAN)
    summed = jnp.dot(picker, stacked, preferred_element_type=jnp.float32)
    dedispersed = summed * subbands ** (-0.5)
    block_count = samples // BLOCK
    blocks = dedispersed.reshape(trial_count, block_count, BLOCK)
    source = lax.iota(jnp.int32, block_count)[None, :] + shift_blocks[:, None]
    shifted = jnp.take_along_axis(blocks, jnp.clip(source, 0, block_count - 1)[:, :, None], axis=1)
    shifted = jnp.where((source < block_count)[:, :, None], shifted, jnp.zeros_like(shifted))
    following = jnp.concatenate([shifted[:, 1:], jnp.zeros_like(shifted[:, :1])], axis=1)
    inside, beyond = template_tables(template_len)
    highest = lax.Precision.HIGHEST
    scores = jnp.einsum("jbp,pm->jbm", shifted, inside, precision=highest)
    scores = scores + jnp.einsum("jbp,pm->jbm", following, beyond, precision=highest)
    templates = template_len.shape[0]
    scores = scores.reshape(trial_count, block_count, templates, BLOCK)
    scores = jnp.transpose(scores, (0, 2, 1, 3)).reshape(trial_count, templates, samples)
    return scores


def solution(mesh):
    in_specs = (
        P(("beam", "chan"), None),
        P("chan", None),
        P(None, "chan"),
        P("chan", None),
        P("chan"),
        P(),
    )
    out_specs = P(("beam", "chan"), None, None)
    return jax.shard_map(local, mesh=mesh, in_specs=in_specs, out_specs=out_specs, check_vma=False)
```

profile of v0, /device:TPU:0, one launch (start us, length us, event | category | flops | bytes accessed | tf_op | source)
XLA Modules:
  0.0 69.2 jit_solution(13036041408480131965)
XLA Ops:
  0.0 0.9 %compare_bitcast_fusion = (pred[32,128]{1,0:T(8,128)(4,1)S(1)}, pred[32,128]{1,0:T(8,128)(4,1)S(1)}, pred[32,128]{1,0:T(8,128)(4,1)S(1)}, pred[32,128]{1,0:T(8,1...) fusion(s32[128,32]{0,1:T(8,128)} %param.7), kind=kLoop, calls=%fused_computation.290 | loop fusion | flops 262144 | bytes 278528 | tf_op jit(solution)/shard_map/eq | solution.py:23
  1.1 1.5 %fusion.224 = f32[128,1024]{1,0:T(8,128)S(1)} fusion(pred[128,128]{1,0:T(8,128)(4,1)S(1)} %bitcast.375, f32[128,1024]{1,0:T(8,128)} %param.6), kind=kOutput, calls=%fused_computation.435 | convolution fusion | flops 201326592 | bytes 1064960 | tf_op jit(solution)/shard_map/dot_general | solution.py:26
  3.1 0.5 convolution_add_fusion.63
  7.5 0.5 convolution_add_fusion.55
  8.6 0.5 convolution_add_fusion.53
  9.7 0.5 convolution_add_fusion.51
  10.2 0.5 convolution_add_fusion.50
  10.8 0.5 convolution_add_fusion.49
  11.3 0.5 convolution_add_fusion.48
  11.9 0.5 convolution_add_fusion.47
  12.9 0.5 convolution_add_fusion.46
  15.6 0.5 convolution_add_fusion.41
  16.7 0.7 %convolution_add_fusion.39 = f32[128,1024]{1,0:T(8,128)S(1)} fusion(f32[128,1024]{1,0:T(8,128)S(1)} %convolution_add_fusion.40, pred[128,128]{1,0:T(8,128)(4,1)S(1)} %bitcast.353, f32[128,1024]{1,0:T(8,128)S(1)} %copy-done), kind=kOutput, calls=%fused_computation.43 | convolution fusion | flops 201457664 | bytes 1589248 | tf_op jit(solution)/shard_map/dot_general | solution.py:26
  17.4 0.5 convolution_add_fusion.38
  18.0 0.5 convolution_add_fusion.37
  18.5 0.5 convolution_add_fusion.36
  19.6 0.5 convolution_add_fusion.34
  20.7 0.5 convolution_add_fusion.32
  21.2 0.5 convolution_add_fusion.31
  21.8 0.5 convolution_add_fusion.30
  22.8 0.5 convolution_add_fusion.29
  25.5 0.5 convolution_add_fusion.24
  26.6 0.5 convolution_add_fusion.22
  27.7 0.5 convolution_add_fusion.20
  28.3 0.5 convolution_add_fusion.19
  29.4 0.5 convolution_add_fusion.17
  30.5 0.5 convolution_add_fusion.15
  31.0 0.5 convolution_add_fusion.14
  31.6 0.5 convolution_add_fusion.13
  32.1 0.8 %convolution_add_fusion.12 = f32[128,1024]{1,0:T(8,128)S(1)} fusion(f32[128,1024]{1,0:T(8,128)S(1)} %convolution_add_fusion.13, pred[128,128]{1,0:T(8,128)(4,1)S(1)} %bitcast.321, f32[128,1024]{1,0:T(8,128)S(1)} %copy-done), kind=kOutput, calls=%fused_computation.16 | convolution fusion | flops 201457664 | bytes 1589248 | tf_op jit(solution)/shard_map/dot_general | solution.py:26
  34.5 0.5 convolution_add_fusion.8
  35.6 0.5 convolution_add_fusion.6
  36.7 0.5 convolution_add_fusion.4
  37.2 0.5 convolution_add_fusion.3
  37.8 0.5 convolution_add_fusion.2
  38.3 0.6 fusion.2
  39.0 0.6 copy-done.2
  39.9 2.8 %gather_fusion = bf16[256,1024]{1,0:T(8,128)(2,1)S(1)} fusion(bf16[32,4,1024]{2,1,0:T(4,128)(2,1)S(1)} %reshape.546, s32[256]{0:T(256)S(1)} %reshape.551), kind=kCustom, calls=%fused_computation | custom fusion | bytes 1050624 | tf_op jit(solution)/shard_map/gather | solution.py:51
  42.7 1.0 %reshape.554 = bf16[16,4,4,1024]{3,2,1,0:T(4,128)(2,1)} reshape(bf16[256,1024]{1,0:T(8,128)(2,1)S(1)} %gather_fusion) | data formatting | bytes 1048576 | tf_op jit(solution)/shard_map/gather | solution.py:51
  43.6 7.4 %all-to-all-start = ((bf16[16,4,4,1024]{3,2,1,0:T(4,128)(2,1)}), bf16[16,4,4,1024]{3,2,1,0:T(4,128)(2,1)S(1)}, u32[]{:S(2)}, u32[]{:S(2)}) async-start(bf16[16,4,4,1024]{3,2,1,0:T(4,128)(2,1)} %reshape.554), calls=%async_computation | async-start | bytes 1048576 | tf_op jit(solution)/shard_map/all_to_all | solution.py:52
  51.1 0.7 copy-done.1
  51.9 0.6 copy-done.3
  52.6 0.6 copy-done.4
  53.5 11.9 %all-to-all-done = bf16[16,4,4,1024]{3,2,1,0:T(4,128)(2,1)S(1)} async-done(((bf16[16,4,4,1024]{3,2,1,0:T(4,128)(2,1)}), bf16[16,4,4,1024]{3,2,1,0:T(4,128)(2,1)S(1)}, u32[]{:S(2)}, u32[]{:S(2)}) %all-to-all-start) | async-done | bytes 524320 | tf_op jit(solution)/shard_map/all_to_all | solution.py:52
  65.7 1.0 %gather_fusion.1 = f32[128,128]{1,0:T(8,128)S(1)} fusion(f32[16,8,128]{2,1,0:T(8,128)S(1)} %bitcast.308, s32[128]{0:T(128)S(1)} %reshape.557), kind=kCustom, calls=%fused_computation.1 | custom fusion | bytes 132096 | tf_op jit(solution)/shard_map/jit(take_along_axis)/gather | solution.py:61
  66.9 0.7 fusion.5
  67.6 0.7 fusion
  68.3 0.9 %reshape.550 = f32[16,8,1024]{2,1,0:T(8,128)} reshape(f32[16,8,8,128]{3,2,1,0:T(8,128)S(1)} %fusion) | data formatting | bytes 1048576 | tf_op jit(solution)/shard_map/reshape | solution.py:70
  (64 shorter events, 18.8 us)
Async XLA Ops:
  1.1 2.0 %copy-start = (f32[128,1024]{1,0:T(8,128)S(1)}, f32[128,1024]{1,0:T(8,128)}, u32[]{:S(2)}) copy-start(f32[128,1024]{1,0:T(8,128)} %param.6) | copy-start | bytes 1572868
  38.9 0.7 copy-start.2
  43.6 21.7 %all-to-all-start = ((bf16[16,4,4,1024]{3,2,1,0:T(4,128)(2,1)}), bf16[16,4,4,1024]{3,2,1,0:T(4,128)(2,1)S(1)}, u32[]{:S(2)}, u32[]{:S(2)}) async-start(bf16[16,4,4,1024]{3,2,1,0:T(4,128)(2,1)} %reshape.554), calls=%async_computation | async-start | bytes 1048576 | tf_op jit(solution)/shard_map/all_to_all | solution.py:52
  51.1 0.7 %copy-start.1 = (s32[16,64]{1,0:T(8,128)S(1)}, s32[16,64]{1,0:T(8,128)}, u32[]{:S(2)}) copy-start(s32[16,64]{1,0:T(8,128)} %param.9) | copy-start | bytes 12292
  51.8 0.7 copy-start.3
  52.5 0.7 copy-start.4
where the time goes:
time: 69.6 us; the launch traced here: 69.2 us
  matrix products  37.5 us (54%)
  waiting for transfers between devices  11.9 us (17%)
  local copies, waits for them, and re-layouts  8.86 us (13%)
  starting transfers between devices  7.41 us (11%)
  other arithmetic  2.89 us (4%)
  between operations  0.73 us (1%)
    dot_general x64, matrix products, make_rows(): jnp.dot(table, moved, precision=highest, preferred_element_type=jnp.float32)  35.9 us
    all_to_all x1, waiting for transfers between devices, local(): lax.all_to_all(windows, 'chan', split_axis=0, concat_axis=0, tiled=True)  11.9 us
    all_to_all x1, starting transfers between devices, local(): lax.all_to_all(windows, 'chan', split_axis=0, concat_axis=0, tiled=True)  7.41 us
    gather x2, local copies, waits for them, and re-layouts, local(): windows = delay_rows[windows_index, band_index]  3.75 us
    unnamed x13, local copies, waits for them, and re-layouts  2.57 us
    and x4, other arithmetic, make_rows(): table = (delay_of == delay)[:, None, :] & same_band[None, :, :]  1.58 us
  transfers between devices with their start and end apart: 1, of which 1 were waited for; matrix products, arithmetic and copies ran while one was open for 1% of the time, Pallas kernels for 0%

commit v1 on v0

v1 whole, which is shorter than its diff:
```python
import functools

import jax
import jax.numpy as jnp
from jax import lax
from jax.experimental import pallas as pl
from jax.experimental.pallas import tpu as pltpu
from jax.sharding import PartitionSpec as P

SUB_CH = 32
NDELAY = 32
MAXD = 64
SPAN = 4
BLOCK = 128
FINE = 8
COARSE = MAXD // FINE


def later(x, amount):
    if amount == 0:
        return x
    moved = pltpu.roll(x, amount, 1)
    lane = lax.broadcasted_iota(jnp.int32, (x.shape[0], BLOCK), 1)
    first = jnp.where(lane >= amount, moved[:, :BLOCK], 0.0)
    return jnp.concatenate([first, moved[:, BLOCK:]], axis=1)


def rows_kernel(spectra_ref, delay_ref, base_ref, out_ref, high_ref, low_ref, sums_ref, rows_ref):
    channels, samples = spectra_ref.shape
    bands = channels // SUB_CH
    owners = base_ref.shape[0]
    delay_of = jnp.transpose(delay_ref[...])
    lane = lax.broadcasted_iota(jnp.int32, (NDELAY, channels), 1)
    fine_per_tile = channels // SUB_CH
    for band in range(bands):
        mine = spectra_ref[band * SUB_CH : (band + 1) * SUB_CH, :]
        for fine in range(FINE):
            moved = later(mine, fine)
            high = moved.astype(jnp.bfloat16)
            low = (moved - high.astype(jnp.float32)).astype(jnp.bfloat16)
            high_ref[fine * SUB_CH : (fine + 1) * SUB_CH, :] = high
            low_ref[fine * SUB_CH : (fine + 1) * SUB_CH, :] = low
        tiled = jnp.where(lane // SUB_CH == band, delay_of, 0)
        step = SUB_CH
        while step < channels:
            tiled = tiled + pltpu.roll(tiled, step, 1)
            step *= 2
        tables = []
        for coarse in range(COARSE):
            parts = []
            for start in range(0, FINE, fine_per_tile):
                wanted = coarse * FINE + start + lane // SUB_CH
                parts.append(jnp.where(tiled == wanted, 1.0, 0.0).astype(jnp.bfloat16))
            tables.append(jnp.concatenate(parts, axis=1))
        table = jnp.concatenate(tables, axis=0)
        sums_ref[...] = jnp.dot(table, high_ref[...], preferred_element_type=jnp.float32) + jnp.dot(
            table, low_ref[...], preferred_element_type=jnp.float32
        )
        total = sums_ref[:NDELAY, :]
        for coarse in range(1, COARSE):
            total = total + later(sums_ref[coarse * NDELAY : (coarse + 1) * NDELAY, :], coarse * FINE)
        rows_ref[band * NDELAY : (band + 1) * NDELAY, :] = (total * SUB_CH ** (-0.5)).astype(jnp.bfloat16)
    width = bands * NDELAY
    lane = lax.broadcasted_iota(jnp.int32, (owners, width), 1)
    base = jnp.zeros((owners, width), jnp.int32)
    for band in range(bands):
        base = jnp.where(lane // NDELAY == band, base_ref[:, band : band + 1], base)
    count = bands * SPAN
    lane = lax.broadcasted_iota(jnp.int32, (count, width), 1)
    place = lax.broadcasted_iota(jnp.int32, (count, width), 0)
    within = jnp.where(place // SPAN == lane // NDELAY, lane % NDELAY - place % SPAN, -1)
    group = min(owners, 16)
    rows = rows_ref[...]
    for start in range(0, owners, group):
        picks = [jnp.where(base[o : o + 1, :] == within, 1.0, 0.0).astype(jnp.bfloat16) for o in range(start, start + group)]
        picked = jnp.dot(jnp.concatenate(picks, axis=0), rows, preferred_element_type=jnp.float32)
        out_ref[start * count : (start + group) * count, :] = picked.astype(jnp.bfloat16)


def column(row, size):
    same = lax.broadcasted_iota(jnp.int32, (size, size), 0) == lax.broadcasted_iota(jnp.int32, (size, size), 1)
    return jnp.sum(jnp.where(same, row.astype(jnp.float32), 0.0), axis=1, keepdims=True).astype(jnp.int32)


def scores_kernel(stacked_ref, offset_ref, shift_ref, length_ref, out_ref, prefix_ref, after_ref):
    trials, subbands = offset_ref.shape
    samples = stacked_ref.shape[1]
    blocks = samples // BLOCK
    templates = length_ref.shape[1]
    spread = lax.broadcasted_iota(jnp.int32, (subbands, subbands * SPAN), 1) // SPAN
    spread = (spread == lax.broadcasted_iota(jnp.int32, (subbands, subbands * SPAN), 0)).astype(jnp.bfloat16)
    wide = jnp.dot(offset_ref[...].astype(jnp.bfloat16), spread, preferred_element_type=jnp.float32)
    span_of = (lax.broadcasted_iota(jnp.int32, wide.shape, 1) % SPAN).astype(jnp.float32)
    picker = jnp.where(wide == span_of, 1.0, 0.0).astype(jnp.bfloat16)
    summed = jnp.dot(picker, stacked_ref[...], preferred_element_type=jnp.float32) * subbands ** (-0.5)
    current = [summed[:, b * BLOCK : (b + 1) * BLOCK] for b in range(blocks)]
    shift = jnp.broadcast_to(column(shift_ref[...], trials), (trials, BLOCK))
    bit = 1
    while bit < blocks:
        taken = (shift & bit) != 0
        current = [jnp.where(taken, current[b + bit] if b + bit < blocks else 0.0, current[b]) for b in range(blocks)]
        bit *= 2
    lane = lax.broadcasted_iota(jnp.int32, (trials, BLOCK), 1)
    before = jnp.zeros((trials, BLOCK), jnp.float32)
    for b in range(blocks):
        total = current[b]
        step = 1
        while step < BLOCK:
            total = total + jnp.where(lane >= step, pltpu.roll(total, step, 1), 0.0)
            step *= 2
        exclusive = total - current[b]
        prefix_ref[:, b * BLOCK : (b + 1) * BLOCK] = exclusive
        if b > 0:
            after_ref[:, (b - 1) * BLOCK : b * BLOCK] = exclusive + before
        before = jnp.broadcast_to(total[:, BLOCK - 1 :], (trials, BLOCK))
    after_ref[:, (blocks - 1) * BLOCK :] = before
    length = jnp.broadcast_to(column(length_ref[...], templates), (templates, BLOCK))
    lane = lax.broadcasted_iota(jnp.int32, (templates, BLOCK), 1)
    source = (lane + length) % BLOCK
    from_next = lane < length
    weight = lax.rsqrt(length.astype(jnp.float32))
    for b in range(blocks):
        for j in range(trials):
            here = jnp.broadcast_to(prefix_ref[j : j + 1, b * BLOCK : (b + 1) * BLOCK], (templates, BLOCK))
            there = jnp.broadcast_to(after_ref[j : j + 1, b * BLOCK : (b + 1) * BLOCK], (templates, BLOCK))
            ends = jnp.take_along_axis(jnp.where(from_next, there, here), source, axis=1)
            out_ref[j, :, b * BLOCK : (b + 1) * BLOCK] = (ends - here) * weight


def local(spectra, chan_delay, window_base, trial_offset, shift_blocks, template_len):
    channels, samples = spectra.shape
    owners = window_base.shape[0]
    bands = channels // SUB_CH
    trials, subbands = trial_offset.shape
    templates = template_len.shape[0]
    count = bands * SPAN
    windows = pl.pallas_call(
        rows_kernel,
        out_shape=jax.ShapeDtypeStruct((owners * count, samples), jnp.bfloat16),
        scratch_shapes=[
            pltpu.VMEM((FINE * SUB_CH, samples), jnp.bfloat16),
            pltpu.VMEM((FINE * SUB_CH, samples), jnp.bfloat16),
            pltpu.VMEM((COARSE * NDELAY, samples), jnp.float32),
            pltpu.VMEM((bands * NDELAY, samples), jnp.bfloat16),
        ],
        name="rows",
    )(spectra, chan_delay, window_base)
    stacked = lax.all_to_all(windows, "chan", split_axis=0, concat_axis=0, tiled=True)
    return pl.pallas_call(
        scores_kernel,
        out_shape=jax.ShapeDtypeStruct((trials, templates, samples), jnp.float32),
        scratch_shapes=[pltpu.VMEM((trials, samples), jnp.float32), pltpu.VMEM((trials, samples), jnp.float32)],
        name="scores",
    )(stacked, trial_offset, shift_blocks.reshape(1, trials), template_len.reshape(1, templates))


def solution(mesh):
    in_specs = (
        P(("beam", "chan"), None),
        P("chan", None),
        P(None, "chan"),
        P("chan", None),
        P("chan"),
        P(),
    )
    out_specs = P(("beam", "chan"), None, None)
    return jax.shard_map(local, mesh=mesh, in_specs=in_specs, out_specs=out_specs, check_vma=False)
```

time: 69.6 us -> 33 us (0.47)
  matrix products: 37.5 us -> 0 us
  blocking collectives: 0 us -> 21.8 us
  waiting for transfers between devices: 11.9 us -> 0 us
  Pallas kernels: 0 us -> 8.06 us
  starting transfers between devices: 7.41 us -> 0 us
  local copies, waits for them, and re-layouts: 8.86 us -> 2.78 us
  other arithmetic: 2.89 us -> 0 us
  between operations: 0.73 us -> 0.01 us
    dot_general x67 -> x0, matrix products: 37.5 us -> none  [the longest x64 35.9 us: make_rows(): jnp.dot(table, moved, precision=highest, preferred_element_type=jnp.float32)]
    all_to_all x0 -> x1, blocking collectives: none -> 21.8 us  [local(): lax.all_to_all(windows, 'chan', split_axis=0, concat_axis=0, tiled=True)]
    all_to_all x1 -> x0, waiting for transfers between devices: 11.9 us -> none  [local(): lax.all_to_all(windows, 'chan', split_axis=0, concat_axis=0, tiled=True)]
    pallas_call x0 -> x2, Pallas kernels: none -> 8.06 us  [the longest x1 5.13 us: local(): pl.pallas_call(rows_kernel, out_shape=jax.ShapeDtypeStruct((owners * coun...]
    all_to_all x1 -> x0, starting transfers between devices: 7.41 us -> none  [local(): lax.all_to_all(windows, 'chan', split_axis=0, concat_axis=0, tiled=True)]
    gather x4 -> x0, local copies, waits for them, and re-layouts: 4.8 us -> none  [the longest x2 3.75 us: local(): windows = delay_rows[windows_index, band_index]]
    and x4 -> x0, other arithmetic: 1.58 us -> none  [make_rows(): table = (delay_of == delay)[:, None, :] & same_band[None, :, :]]
    reshape x3 -> x0, local copies, waits for them, and re-layouts: 1.1 us -> none  [the longest x1 0.88 us: local(): jnp.transpose(scores, (0, 2, 1, 3)).reshape(trial_count, templates, samples)]
  transfers between devices with their start and end apart: 1 -> 0, of which waited for: 1 -> 0; matrix products, arithmetic and copies ran while one was open for 1% -> 0% of each run, Pallas kernels for 0% -> 0%
where the time goes in v1:
time: 33 us; the launch traced here: 32.6 us
  blocking collectives  21.8 us (66%)
  Pallas kernels  8.06 us (24%)
  local copies, waits for them, and re-layouts  2.78 us (8%)
    all_to_all x1, blocking collectives, local(): lax.all_to_all(windows, 'chan', split_axis=0, concat_axis=0, tiled=True)  21.8 us
    pallas_call x1, Pallas kernels, local(): pl.pallas_call(rows_kernel, out_shape=jax.ShapeDtypeStruct((owners * coun...  5.13 us
    pallas_call x1, Pallas kernels, local(): pl.pallas_call(scores_kernel, out_shape=jax.ShapeDtypeStruct((trials, tem...  2.94 us
    unnamed x2, local copies, waits for them, and re-layouts  2.78 us

profile of v1, /device:TPU:0, one launch (start us, length us, event | category | flops | bytes accessed | tf_op | source)
XLA Modules:
  0.0 32.6 jit_solution(6700928834908383104)
XLA Ops:
  0.0 1.3 %copy.8.base_ref = s32[16,4]{1,0:T(8,128)} copy(s32[16,4]{0,1:T(4,128)} %param.8) | data formatting | bytes 512 | tf_op args[2]
  1.4 1.4 %copy.7.delay_ref = s32[128,32]{1,0:T(8,128)} copy(s32[128,32]{0,1:T(8,128)} %param.7) | data formatting | bytes 32768 | tf_op args[1]
  2.8 5.1 %rows.1 = bf16[256,1024]{1,0:T(8,128)(2,1)} custom-call(f32[128,1024]{1,0:T(8,128)} %spectra_ref.1, s32[128,32]{1,0:T(8,128)} %copy.7.delay_ref, s32[16,4]{1,0:T(8,128)} %copy.8.base_ref), custom_call_target="tpu_custom_call" | custom-call | tf_op jit(solution)/shard_map/rows/pallas_call | solution.py:137
  7.9 21.8 %all_to_all.11 = bf16[16,16,1024]{2,1,0:T(8,128)(2,1)} all-to-all(bf16[16,16,1024]{2,1,0:T(8,128)(2,1)} %bitcast.5), channel_id=1, replica_groups=mesh['beam'=2,'chan'=16] {'chan'}, dimensions={0} | all-to-all | bytes 1048576 | tf_op jit(solution)/shard_map/all_to_all | solution.py:148
  29.7 2.9 %scores.1 = f32[16,8,1024]{2,1,0:T(8,128)} custom-call(bf16[256,1024]{1,0:T(8,128)(2,1)} %bitcast.4, s32[16,64]{1,0:T(8,128)} %offset_ref.1, s32[1,16]{1,0:T(1,128)} %bitcast.6, s32[1,8]{1,0:T(1,128)} %bitcast.7), custom_call_target="tpu_custom_call" | custom-call | tf_op jit(solution)/shard_map/scores/pallas_call | solution.py:149

commit v2 on v1

v2 whole, which is shorter than its diff:
```python
import jax
import jax.numpy as jnp
from jax import lax
from jax.experimental import pallas as pl
from jax.experimental.pallas import tpu as pltpu
from jax.sharding import PartitionSpec as P

SUB_CH = 32
NDELAY = 32
MAXD = 64
SPAN = 4
BLOCK = 128
FINE = 8
COARSE = MAXD // FINE
TILE = 256
HALF = 16


def later(x, amount):
    if amount == 0:
        return x
    moved = pltpu.roll(x, amount, 1)
    lane = lax.broadcasted_iota(jnp.int32, (x.shape[0], BLOCK), 1)
    first = jnp.where(lane >= amount, moved[:, :BLOCK], jnp.zeros((), x.dtype))
    return jnp.concatenate([first, moved[:, BLOCK:]], axis=1)


def column(row, size):
    same = lax.broadcasted_iota(jnp.int32, (size, size), 0) == lax.broadcasted_iota(jnp.int32, (size, size), 1)
    return jnp.sum(jnp.where(same, row.astype(jnp.float32), 0.0), axis=1, keepdims=True).astype(jnp.int32)


def rows_kernel(
    spectra_hbm, delay_hbm, base_hbm, offset_hbm, shift_hbm, length_hbm,
    windows_ref, picker_ref, shift_ref, length_ref,
    spectra_ref, delay_ref, base_ref, offset_in, shift_in, length_in,
    tables_ref, picks_ref, terms_ref, sums_ref, rows_ref, sems,
):
    channels, samples = spectra_ref.shape
    bands = channels // SUB_CH
    owners = base_ref.shape[1]
    depth = FINE * SUB_CH
    width = bands * NDELAY
    count = bands * SPAN

    small = [
        pltpu.make_async_copy(source, target, sems.at[bands + i])
        for i, (source, target) in enumerate(
            [(delay_hbm, delay_ref), (base_hbm, base_ref), (offset_hbm, offset_in), (shift_hbm, shift_in), (length_hbm, length_in)]
        )
    ]
    large = []
    for band in range(bands):
        part = pl.ds(band * SUB_CH, SUB_CH)
        large.append(pltpu.make_async_copy(spectra_hbm.at[part], spectra_ref.at[part], sems.at[band]))
    small[0].start()
    for copy in large:
        copy.start()
    for copy in small[1:]:
        copy.start()

    small[0].wait()
    lane = lax.broadcasted_iota(jnp.int32, (NDELAY, channels), 1)
    for band in range(bands):
        tiled = jnp.where(lane // SUB_CH == band, delay_ref[...], 0)
        step = SUB_CH
        while step < channels:
            tiled = tiled + pltpu.roll(tiled, step, 1)
            step *= 2
        for coarse in range(COARSE):
            for start in range(0, FINE, bands):
                wanted = coarse * FINE + start + lane // SUB_CH
                table = jnp.where(tiled == wanted, 1.0, 0.0).astype(jnp.bfloat16)
                tables_ref[band, coarse * NDELAY : (coarse + 1) * NDELAY, start * SUB_CH : start * SUB_CH + channels] = table

    def fill(band, fine):
        slot = band % 2
        for start in range(0, SUB_CH, HALF):
            at = fine * SUB_CH + start
            if fine == 0:
                first = spectra_ref[band * SUB_CH + start : band * SUB_CH + start + HALF, :]
                high = first.astype(jnp.bfloat16)
                low = (first - high.astype(jnp.float32)).astype(jnp.bfloat16)
            else:
                high = later(terms_ref[slot, start : start + HALF, :], fine)
                low = later(terms_ref[slot, depth + start : depth + start + HALF, :], fine)
            terms_ref[slot, at : at + HALF, :] = high
            terms_ref[slot, depth + at : depth + at + HALF, :] = low

    def multiply(band, tile):
        slot = band % 2
        table = tables_ref[band]
        both = jnp.concatenate([table, table], axis=1)
        columns = slice(tile * TILE, (tile + 1) * TILE)
        sums_ref[slot, :, columns] = jnp.dot(both, terms_ref[slot, :, columns], preferred_element_type=jnp.float32)

    def drain(band, start):
        slot = band % 2
        total = sums_ref[slot, start : start + HALF, :]
        for coarse in range(1, COARSE):
            at = coarse * NDELAY + start
            total = total + later(sums_ref[slot, at : at + HALF, :], coarse * FINE)
        rows_ref[band * NDELAY + start : band * NDELAY + start + HALF, :] = (total * SUB_CH ** (-0.5)).astype(jnp.bfloat16)

    tiles = samples // TILE
    for step in range(bands + 2):
        if step < bands:
            large[step].wait()
        for tile in range(tiles):
            if step < bands:
                for fine in range(tile * FINE // tiles, (tile + 1) * FINE // tiles):
                    fill(step, fine)
            if 1 <= step <= bands:
                multiply(step - 1, tile)
            if step >= 2:
                for start in range(0, NDELAY, HALF):
                    if (start // HALF + 1) * tiles // (NDELAY // HALF) - 1 == tile:
                        drain(step - 2, start)
        if step == 0:
            small[1].wait()
            base_of = jnp.transpose(base_ref[...])
            lane = lax.broadcasted_iota(jnp.int32, (owners, width), 1)
            base = jnp.zeros((owners, width), jnp.int32)
            for band in range(bands):
                base = jnp.where(lane // NDELAY == band, base_of[:, band : band + 1], base)
            lane = lax.broadcasted_iota(jnp.int32, (count, width), 1)
            place = lax.broadcasted_iota(jnp.int32, (count, width), 0)
            within = jnp.where(place // SPAN == lane // NDELAY, lane % NDELAY - place % SPAN, -1)
            for owner in range(owners):
                pick = jnp.where(base[owner : owner + 1, :] == within, 1.0, 0.0)
                picks_ref[owner * count : (owner + 1) * count, :] = pick.astype(jnp.bfloat16)
        if step == 1:
            small[2].wait()
            small[3].wait()
            small[4].wait()
            subbands = offset_in.shape[1]
            spread = lax.broadcasted_iota(jnp.int32, (subbands, subbands * SPAN), 1) // SPAN
            spread = (spread == lax.broadcasted_iota(jnp.int32, (subbands, subbands * SPAN), 0)).astype(jnp.bfloat16)
            wide = jnp.dot(offset_in[...].astype(jnp.bfloat16), spread, preferred_element_type=jnp.float32)
            span_of = (lax.broadcasted_iota(jnp.int32, wide.shape, 1) % SPAN).astype(jnp.float32)
            picker_ref[...] = jnp.where(wide == span_of, 1.0, 0.0).astype(jnp.bfloat16)
            shift_ref[...] = jnp.broadcast_to(column(shift_in[...], shift_ref.shape[0]), shift_ref.shape)
            length_ref[...] = jnp.broadcast_to(column(length_in[...], length_ref.shape[0]), length_ref.shape)

    total = owners * count
    group = min(total, TILE)
    for start in range(0, total, group):
        for tile in range(tiles):
            columns = slice(tile * TILE, (tile + 1) * TILE)
            picked = jnp.dot(picks_ref[start : start + group, :], rows_ref[:, columns], preferred_element_type=jnp.float32)
            windows_ref[start : start + group, columns] = picked.astype(jnp.bfloat16)


def scores_kernel(stacked_ref, picker_ref, shift_ref, length_ref, out_hbm, prefix_ref, after_ref, out_ref, sems):
    trials, templates, samples = out_ref.shape
    blocks = samples // BLOCK
    subbands = picker_ref.shape[1] // SPAN
    summed = jnp.dot(picker_ref[...], stacked_ref[...], preferred_element_type=jnp.float32) * subbands ** (-0.5)
    current = [summed[:, b * BLOCK : (b + 1) * BLOCK] for b in range(blocks)]
    shift = shift_ref[...]
    bit = 1
    while bit < blocks:
        taken = (shift & bit) != 0
        current = [jnp.where(taken, current[b + bit] if b + bit < blocks else 0.0, current[b]) for b in range(blocks)]
        bit *= 2
    whole = jnp.concatenate(current, axis=0)
    high = whole.astype(jnp.bfloat16)
    rest = whole - high.astype(jnp.float32)
    middle = rest.astype(jnp.bfloat16)
    low = (rest - middle.astype(jnp.float32)).astype(jnp.bfloat16)
    row = lax.broadcasted_iota(jnp.int32, (BLOCK, 2 * BLOCK), 0)
    lane = lax.broadcasted_iota(jnp.int32, (BLOCK, 2 * BLOCK), 1)
    ones = jnp.where((row < lane) | (lane >= BLOCK), 1.0, 0.0).astype(jnp.bfloat16)
    both = jnp.dot(
        jnp.concatenate([high, middle, low], axis=1), jnp.concatenate([ones, ones, ones], axis=0), preferred_element_type=jnp.float32
    )
    for b in range(blocks):
        columns = slice(b * BLOCK, (b + 1) * BLOCK)
        prefix_ref[:, columns] = both[b * trials : (b + 1) * trials, :BLOCK]
        after = both[b * trials : (b + 1) * trials, BLOCK:]
        if b + 1 < blocks:
            after = after + both[(b + 1) * trials : (b + 2) * trials, :BLOCK]
        after_ref[:, columns] = after
    length = length_ref[...]
    lane = lax.broadcasted_iota(jnp.int32, (templates, BLOCK), 1)
    source = (lane + length) % BLOCK
    from_next = lane < length
    weight = lax.rsqrt(length.astype(jnp.float32))
    chunk = trials // sems.shape[0]
    copies = []
    for j in range(trials):
        for b in range(blocks):
            columns = slice(b * BLOCK, (b + 1) * BLOCK)
            here = jnp.broadcast_to(prefix_ref[j : j + 1, columns], (templates, BLOCK))
            there = jnp.broadcast_to(after_ref[j : j + 1, columns], (templates, BLOCK))
            ends = jnp.take_along_axis(jnp.where(from_next, there, here), source, axis=1)
            out_ref[j, :, columns] = (ends - here) * weight
        if (j + 1) % chunk == 0:
            part = pl.ds(j + 1 - chunk, chunk)
            copies.append(pltpu.make_async_copy(out_ref.at[part], out_hbm.at[part], sems.at[len(copies)]))
            copies[-1].start()
    for copy in copies:
        copy.wait()


def local(spectra, chan_delay, window_base, trial_offset, shift_blocks, template_len):
    channels, samples = spectra.shape
    owners = window_base.shape[0]
    bands = channels // SUB_CH
    trials, subbands = trial_offset.shape
    templates = template_len.shape[0]
    count = bands * SPAN
    depth = FINE * SUB_CH
    anywhere = pl.BlockSpec(memory_space=pltpu.HBM)
    inside = pl.BlockSpec(memory_space=pltpu.VMEM)
    limits = pltpu.CompilerParams(vmem_limit_bytes=24 * 1024 * 1024)
    arrays = (spectra, chan_delay.T, window_base.T, trial_offset, shift_blocks.reshape(1, trials), template_len.reshape(1, templates))
    windows, picker, shift, length = pl.pallas_call(
        rows_kernel,
        out_shape=(
            pltpu.VMEM((owners * count, samples), jnp.bfloat16),
            pltpu.VMEM((trials, subbands * SPAN), jnp.bfloat16),
            pltpu.VMEM((trials, BLOCK), jnp.int32),
            pltpu.VMEM((templates, BLOCK), jnp.int32),
        ),
        in_specs=[anywhere] * 6,
        scratch_shapes=[
            pltpu.VMEM((channels, samples), jnp.float32),
            pltpu.VMEM((NDELAY, channels), jnp.int32),
            pltpu.VMEM((bands, owners), jnp.int32),
            pltpu.VMEM((trials, subbands), jnp.int32),
            pltpu.VMEM((1, trials), jnp.int32),
            pltpu.VMEM((1, templates), jnp.int32),
            pltpu.VMEM((bands, COARSE * NDELAY, depth), jnp.bfloat16),
            pltpu.VMEM((owners * count, bands * NDELAY), jnp.bfloat16),
            pltpu.VMEM((2, 2 * depth, samples), jnp.bfloat16),
            pltpu.VMEM((2, COARSE * NDELAY, samples), jnp.float32),
            pltpu.VMEM((bands * NDELAY, samples), jnp.bfloat16),
            pltpu.SemaphoreType.DMA((bands + 5,)),
        ],
        compiler_params=limits,
        name="rows",
    )(*(pltpu.with_memory_space_constraint(array, pltpu.HBM) for array in arrays))
    stacked = lax.all_to_all(windows, "chan", split_axis=0, concat_axis=0, tiled=True)
    stacked = pltpu.with_memory_space_constraint(stacked, pltpu.VMEM)
    return pl.pallas_call(
        scores_kernel,
        out_shape=jax.ShapeDtypeStruct((trials, templates, samples), jnp.float32),
        in_specs=[inside] * 4,
        out_specs=anywhere,
        scratch_shapes=[
            pltpu.VMEM((trials, samples), jnp.float32),
            pltpu.VMEM((trials, samples), jnp.float32),
            pltpu.VMEM((trials, templates, samples), jnp.float32),
            pltpu.SemaphoreType.DMA((4,)),
        ],
        compiler_params=limits,
        name="scores",
    )(stacked, picker, shift, length)


def solution(mesh):
    in_specs = (
        P(("beam", "chan"), None),
        P("chan", None),
        P(None, "chan"),
        P("chan", None),
        P("chan"),
        P(),
    )
    out_specs = P(("beam", "chan"), None, None)
    return jax.shard_map(local, mesh=mesh, in_specs=in_specs, out_specs=out_specs, check_vma=False)
```

time: 33 us -> 27.2 us (0.82)
  local copies, waits for them, and re-layouts: 2.78 us -> 0 us
  Pallas kernels: 8.06 us -> 5.41 us
    unnamed x2 -> x0, local copies, waits for them, and re-layouts: 2.78 us -> none
    pallas_call x1, Pallas kernels: 2.94 us -> 1.39 us  [local(): pl.pallas_call(scores_kernel, out_shape=jax.ShapeDtypeStruct((trials, tem...]
    pallas_call x1, Pallas kernels: 5.13 us -> 4.03 us  [local(): pl.pallas_call(rows_kernel, out_shape=(pltpu.VMEM((owners * count, sample...]
where the time goes in v2:
time: 27.2 us; the launch traced here: 26.9 us
  blocking collectives  21.5 us (79%)
  Pallas kernels  5.41 us (20%)
    all_to_all x1, blocking collectives, local(): lax.all_to_all(windows, 'chan', split_axis=0, concat_axis=0, tiled=True)  21.5 us
    pallas_call x1, Pallas kernels, local(): pl.pallas_call(rows_kernel, out_shape=(pltpu.VMEM((owners * count, sample...  4.03 us
    pallas_call x1, Pallas kernels, local(): pl.pallas_call(scores_kernel, out_shape=jax.ShapeDtypeStruct((trials, tem...  1.39 us

profile of v2, /device:TPU:0, one launch (start us, length us, event | category | flops | bytes accessed | tf_op | source)
XLA Modules:
  0.0 26.9 jit_solution(8148304129128264478)
XLA Ops:
  0.0 4.0 %rows.1 = (bf16[256,1024]{1,0:T(8,128)(2,1)S(1)}, bf16[16,256]{1,0:T(8,128)(2,1)S(1)}, s32[16,128]{1,0:T(8,128)S(1)}, s32[8,128]{1,0:T(8,128)S(1)}) custom-call(f32[128,1024]{1,0:T(8,128)} %spectra_hbm.1, s32[32,128]{1,0:T(8,128)} %bitcast.8, s32[4,16]{1,0:T(4,128)} %bitcast.9, s32[16,64]{1,0:T(8,128)} %offset_hbm.1, s32[1,16]{1,0:T(1,128)} %bitcast.10, ...), custom_call_target="tpu_custom_call" | custom-call | tf_op jit(solution)/shard_map/rows/pallas_call | solution.py:218
  4.0 21.5 %all_to_all.11 = bf16[16,16,1024]{2,1,0:T(8,128)(2,1)S(1)} all-to-all(bf16[16,16,1024]{2,1,0:T(8,128)(2,1)S(1)} %bitcast.7), channel_id=1, replica_groups=mesh['beam'=2,'chan'=16] {'chan'}, dimensions={0} | all-to-all | bytes 1048576 | tf_op jit(solution)/shard_map/all_to_all | solution.py:244
  25.5 1.4 %scores.1 = f32[16,8,1024]{2,1,0:T(8,128)} custom-call(bf16[256,1024]{1,0:T(8,128)(2,1)S(1)} %bitcast.6, bf16[16,256]{1,0:T(8,128)(2,1)S(1)} %get-tuple-element.10.picker_ref, s32[16,128]{1,0:T(8,128)S(1)} %get-tuple-element.11.shift_ref, s32[8,128]{1,0:T(8,128)S(1)} %get-tuple-element.12.length_ref), custom_call_target="tpu_custom_call" | custom-call | tf_op jit(solution)/shard_map/scores/pallas_call | solution.py:246
